TPU v7x, 32 devices: a whole 2x2x4 slice. The times are simulated.
32 devices in a mesh: rep: 2 (over y), gx: 8 (over z, x), gy: 2 (over core).
Axes of the slice: x: 2, y: 2, z: 4, core: 2. Of those that a mesh axis runs over, the one named last changes fastest.
Arguments:
- tokens: bfloat16 [768, 8192], P(('rep', 'gx'), 'gy'), parts along dimension 0, may hold values from -6 to 6
- segment_ids: int32 [768], P(('rep', 'gx')), parts along dimension 0, may hold values from 0 to 1, as said below
- gate_weight: bfloat16 [8192, 2, 13312], P(None, 'gy', 'gx'), may hold values from -0.0625 to 0.0625
- up_weight: bfloat16 [8192, 2, 13312], P(None, 'gy', 'gx'), may hold values from -0.0625 to 0.0625
- down_weight: bfloat16 [2, 13312, 8192], P('gy', None, 'gx'), may hold values from -0.0390625 to 0.0390625
Outputs:
- grouped: bfloat16 [768, 8192], P(('rep', 'gx'), 'gy'), parts along dimension 0
There are 2 independent parts, one for each index of `rep`. A program takes and returns all parts, laid end to end along the dimension named above; an argument that names none is the same for every part. Nothing has to cross between parts.
Inputs may be any that keep to these rules, and one draw needn't show every extreme that they name: `segment_ids`: exactly 320 entries are 0 and 64 entries are 1.
All inputs are finite; a program needn't handle non-finite values.
Results may differ from a plain program's by a relative error of at most 0.0049.
Values may be sent and summed in bfloat16 or wider, within the bound.
A program may use at most 128 MiB of HBM per device.

v0:
```python
import jax
import jax.numpy as jnp
from jax import lax
from jax.sharding import PartitionSpec as P

PREFILL = 320


def grouped_target(token_kinds):
    decode_flag = token_kinds.astype(jnp.int32)
    prefill_flag = 1 - decode_flag
    prefill_rank = jnp.cumsum(prefill_flag) - 1
    decode_rank = jnp.cumsum(decode_flag) - 1
    return jnp.where(decode_flag == 0, prefill_rank, PREFILL + decode_rank)


def local(tokens, segment_ids, gate_weight, up_weight, down_weight):
    half_rows, token_kinds = (
        lax.all_gather(tokens, "gx", axis=0, tiled=True),
        lax.all_gather(segment_ids, "gx", axis=0, tiled=True),
    )
    gathered = lax.all_gather(half_rows, "gy", axis=1, tiled=True)
    gate_local = gate_weight.reshape(gate_weight.shape[0], -1)
    up_local = up_weight.reshape(up_weight.shape[0], -1)
    down_local = down_weight.reshape(-1, down_weight.shape[2])
    target = grouped_target(token_kinds)
    gate_value = jnp.dot(gathered, gate_local, preferred_element_type=jnp.float32)
    up_value = jnp.dot(gathered, up_local, preferred_element_type=jnp.float32)
    hidden = (jax.nn.silu(gate_value) * up_value).astype(jnp.bfloat16)
    partial_value = jnp.dot(
        lax.all_gather(hidden, "gx", axis=1, tiled=True),
        down_local,
        preferred_element_type=jnp.float32,
    )
    placed = jnp.zeros_like(partial_value).at[target].set(partial_value)
    switched = lax.all_to_all(placed, "gx", split_axis=0, concat_axis=1, tiled=True)
    return lax.psum_scatter(switched, "gy", scatter_dimension=1, tiled=True).astype(jnp.bfloat16)


def solution(mesh):
    placed = (
        P(("rep", "gx"), "gy"),
        P(("rep", "gx")),
        P(None, "gy", "gx"),
        P(None, "gy", "gx"),
        P("gy", None, "gx"),
    )
    return jax.shard_map(
        local, mesh=mesh, in_specs=placed, out_specs=P(("rep", "gx"), "gy"), check_vma=False
    )
```

profile of v0, /device:TPU:0, one launch (start us, length us, event | category | flops | bytes accessed | tf_op | source)
XLA Modules:
  0.0 349.0 jit_solution(17059045087787069002)
XLA Ops:
  6.5 0.0 all-gather.4.cloned.1.call-start
  6.5 0.7 all-gather.4.cloned.1.call-update
  7.3 0.0 all-gather.6.cloned.1.call-start
  7.3 65.0 %all-gather.4.cloned.1.call-done = bf16[384,4096]{1,0:T(8,128)(2,1)} async-done(((bf16[48,4096]{1,0:T(8,128)(2,1)}), bf16[384,4096]{1,0:T(8,128)(2,1)}) %all-gather.4.cloned.1.call-update) | async-done | bytes 3145744 | tf_op jit(solution)/shard_map/all_gather | solution.py:19
  72.3 0.0 all-gather.6.cloned.1.call-update
  72.3 0.0 all-gather.8.cloned.1.call-start
  72.4 16.9 %all-gather.6.cloned.1.call-done = bf16[384,8192]{1,0:T(8,128)(2,1)} async-done(((bf16[384,4096]{1,0:T(8,128)(2,1)}), bf16[384,8192]{1,0:T(8,128)(2,1)}) %all-gather.6.cloned.1.call-update) | async-done | bytes 6291472 | tf_op jit(solution)/shard_map/all_gather | solution.py:22
  89.3 0.0 copy-start
  89.3 17.7 %fusion.4 = f32[384,1664]{1,0:T(8,128)S(1)} fusion(bf16[384,8192]{1,0:T(8,128)(2,1)} %all-gather.6.cloned.1.call-done, bf16[8192,1,1664]{2,0,1:T(8,128)(2,1)} %param.7), kind=kOutput, calls=%fused_computation.5 | convolution fusion | flops 10468982784 | bytes 36110336 | tf_op jit(solution)/shard_map/dot_general | solution.py:27
  107.0 0.0 copy-done
  107.0 0.0 copy-start.2
  107.0 0.0 copy-start.1
  107.0 16.7 %fusion.9 = bf16[384,1664]{1,0:T(8,128)(2,1)} fusion(bf16[384,8192]{1,0:T(8,128)(2,1)S(1)} %copy-done, bf16[8192,1,1664]{2,0,1:T(8,128)(2,1)} %param.8, f32[384,1664]{1,0:T(8,128)S(1)} %fusion.4), kind=kOutput, calls=%fused_computation.8 | convolution fusion | flops 10472816640 | bytes 37388288 | tf_op jit(solution)/shard_map/dot_general | solution.py:28
  123.7 0.0 all-gather.8.cloned.1.call-update
  123.7 0.0 reduce-scatter.2.cloned.1.call-start
  123.8 0.0 copy-done.2
  123.8 0.6 dynamic-slice
  125.0 0.0 copy-done.1
  125.0 0.2 dynamic-update-slice
  125.3 11.6 %all-reduce = s32[384]{0:T(512)S(1)} all-reduce(s32[384]{0:T(512)S(1)} %dynamic-update-slice), channel_id=1, replica_groups=mesh['rep'=2,'gx'=8,'gy'=2] {'gx'}, use_global_device_ids=true, to_apply=%add | all-reduce | flops 384 | bytes 3072
  136.9 0.3 reduce-window.24
  137.2 0.1 slice.16
  137.3 0.3 reduce-window.16
  137.6 0.1 slice.14
  137.8 0.1 slice_reduce_fusion
  137.9 0.1 compare_select_fusion
  138.0 134.0 %all-gather.8.cloned.1.call-done = bf16[384,13312]{1,0:T(8,128)(2,1)} async-done(((bf16[384,1664]{1,0:T(8,128)(2,1)}), bf16[384,13312]{1,0:T(8,128)(2,1)}) %all-gather.8.cloned.1.call-update) | async-done | bytes 10223632 | tf_op jit(solution)/shard_map/all_gather | solution.py:31
  272.0 17.4 %fusion = f32[384,1024]{1,0:T(8,128)S(1)} fusion(bf16[384,13312]{1,0:T(8,128)(2,1)} %all-gather.8.cloned.1.call-done, bf16[1,13312,1024]{2,1,0:T(8,128)(2,1)} %param.9), kind=kOutput, calls=%fused_computation.1 | convolution fusion | flops 10468982784 | bytes 39059456 | tf_op jit(solution)/shard_map/dot_general | solution.py:30
  289.4 2.2 scatter_custom_fusion
  291.6 39.6 %all_to_all.19 = f32[8,48,1024]{2,1,0:T(8,128)S(1)} all-to-all(f32[8,48,1024]{2,1,0:T(8,128)S(1)} %bitcast.32), channel_id=1, replica_groups=mesh['rep'=2,'gx'=8,'gy'=2] {'gx'}, dimensions={0} | all-to-all | bytes 3145728 | tf_op jit(solution)/shard_map/all_to_all | solution.py:36
  331.2 1.3 copy.7
  332.4 0.0 reduce-scatter.2.cloned.1.call-update
  332.4 8.1 %reduce-scatter.2.cloned.1.call-done = f32[48,4096]{1,0:T(8,128)} async-done(((f32[48,8192]{1,0:T(8,128)}), f32[48,4096]{1,0:T(8,128)}) %reduce-scatter.2.cloned.1.call-update) | async-done | bytes 786448 | tf_op jit(solution)/shard_map/reduce_scatter | solution.py:37
  340.5 1.9 convert_element_type.7
  (4 shorter events, 0.1 us)
Async XLA Ops:
  6.5 65.7 %all-gather.4.cloned.1.call-start = ((), (), s32[]{:S(2)}) async-start(), calls=%async_computation.2 | async-start | bytes 3538944 | tf_op jit(solution)/shard_map/all_gather | solution.py:19
  7.3 82.0 %all-gather.6.cloned.1.call-start = ((), (), s32[]{:S(2)}) async-start(), calls=%async_computation.3 | async-start | bytes 9437184 | tf_op jit(solution)/shard_map/all_gather | solution.py:22
  72.3 199.7 %all-gather.8.cloned.1.call-start = ((), (), s32[]{:S(2)}) async-start(), calls=%async_computation.4 | async-start | bytes 11501568 | tf_op jit(solution)/shard_map/all_gather | solution.py:31
  89.3 17.7 %copy-start = (bf16[384,8192]{1,0:T(8,128)(2,1)S(1)}, bf16[384,8192]{1,0:T(8,128)(2,1)}, u32[]{:S(2)}) copy-start(bf16[384,8192]{1,0:T(8,128)(2,1)} %all-gather.6.cloned.1.call-done) | copy-start | bytes 18874372
  107.0 16.8 %copy-start.2 = (u32[32]{0:T(128)S(1)}, u32[32]{0:T(128)}, u32[]{:S(2)}) copy-start(u32[32]{0:T(128)} %constant.26) | copy-start | bytes 388
  107.0 18.0 %copy-start.1 = (s32[48]{0:T(128)S(1)}, s32[48]{0:T(128)}, u32[]{:S(2)}) copy-start(s32[48]{0:T(128)} %param.6) | copy-start | bytes 580
  123.7 216.8 %reduce-scatter.2.cloned.1.call-start = ((), (), s32[]{:S(2)}) async-start(), calls=%async_computation.5 | async-start | bytes 2359296 | tf_op jit(solution)/shard_map/reduce_scatter | solution.py:37
Sparse Core Ops, SparseCore 0:
  9.5 62.7 all-gather.3
  73.8 15.4 all-gather.5
  123.8 148.1 all-gather.7
  332.6 7.9 reduce-scatter.1
where the time goes:
time: 349 us
  waiting for transfers between devices  225 us (64%)
  matrix products  51.7 us (15%)
  blocking collectives  51.2 us (15%)
  between operations  13.9 us (4%)
  local copies, waits for them, and re-layouts  4.61 us (1%)
    all_gather x1, waiting for transfers between devices, local(): lax.all_gather(hidden, 'gx', axis=1, tiled=True)  134 us
    all_gather x1, waiting for transfers between devices, local(): lax.all_gather(tokens, 'gx', axis=0, tiled=True)  65 us
    all_to_all x1, blocking collectives, local(): lax.all_to_all(placed, 'gx', split_axis=0, concat_axis=1, tiled=True)  39.6 us
    dot_general x1, matrix products, local(): jnp.dot(gathered, gate_local, preferred_element_type=jnp.float32)  17.7 us
    dot_general x1, matrix products, local(): jnp.dot(lax.all_gather(hidden, 'gx', axis=1, tiled=True), down_local, pre...  17.4 us
    all_gather x1, waiting for transfers between devices, local(): gathered = lax.all_gather(half_rows, 'gy', axis=1, tiled=True)  16.9 us
    dot_general x1, matrix products, local(): up_value = jnp.dot(gathered, up_local, preferred_element_type=jnp.float32)  16.7 us
    unnamed x1, blocking collectives  11.6 us
  transfers between devices with their start and end apart: 4, of which 4 were waited for; matrix products, arithmetic and copies ran while one was open for 1% of the time, Pallas kernels for 0%

commit v1 on v0

--- a/solution.py
+++ b/solution.py
@@ -16,7 +16,9 @@
 
 def local(tokens, segment_ids, gate_weight, up_weight, down_weight):
     half_rows, token_kinds = (
-        lax.all_gather(tokens, "gx", axis=0, tiled=True),
+        jnp.concatenate(
+            lax.all_to_all(jnp.stack([tokens] * lax.axis_size("gx")), "gx", 0, 0), axis=0
+        ),
         lax.all_gather(segment_ids, "gx", axis=0, tiled=True),
     )
     gathered = lax.all_gather(half_rows, "gy", axis=1, tiled=True)

time: 349 us -> 362 us (1.037)
  blocking collectives: 51.2 us -> 129 us
  waiting for transfers between devices: 225 us -> 158 us
    all_to_all x0 -> x1, blocking collectives: none -> 77.9 us  [local(): lax.all_to_all(jnp.stack([tokens] * lax.axis_size('gx')), 'gx', 0, 0)]
    all_gather x1 -> x0, waiting for transfers between devices: 65 us -> none  [local(): lax.all_gather(tokens, 'gx', axis=0, tiled=True)]
  transfers between devices with their start and end apart: 4 -> 3, of which waited for: 4 -> 3; matrix products, arithmetic and copies ran while one was open for 1% -> 1% of each run, Pallas kernels for 0% -> 0%
where the time goes in v1:
time: 362 us; the launch traced here: 361 us
  waiting for transfers between devices  158 us (44%)
  blocking collectives  129 us (36%)
  matrix products  51.7 us (14%)
  between operations  13.9 us (4%)
  local copies, waits for them, and re-layouts  5.97 us (2%)
    all_gather x1, waiting for transfers between devices, local(): lax.all_gather(hidden, 'gx', axis=1, tiled=True)  134 us
    all_to_all x1, blocking collectives, local(): lax.all_to_all(jnp.stack([tokens] * lax.axis_size('gx')), 'gx', 0, 0)  77.9 us
    all_to_all x1, blocking collectives, local(): lax.all_to_all(placed, 'gx', split_axis=0, concat_axis=1, tiled=True)  39.6 us
    dot_general x1, matrix products, local(): jnp.dot(gathered, gate_local, preferred_element_type=jnp.float32)  17.7 us
    dot_general x1, matrix products, local(): jnp.dot(lax.all_gather(hidden, 'gx', axis=1, tiled=True), down_local, pre...  17.4 us
    dot_general x1, matrix products, local(): up_value = jnp.dot(gathered, up_local, preferred_element_type=jnp.float32)  16.7 us
    all_gather x1, waiting for transfers between devices, local(): gathered = lax.all_gather(half_rows, 'gy', axis=1, tiled=True)  15.9 us
    unnamed x1, blocking collectives  11.6 us
  transfers between devices with their start and end apart: 3, of which 3 were waited for; matrix products, arithmetic and copies ran while one was open for 1% of the time, Pallas kernels for 0%

profile of v1, /device:TPU:0, one launch (start us, length us, event | category | flops | bytes accessed | tf_op | source)
XLA Modules:
  0.0 361.5 jit_solution(18357568223474170661)
XLA Ops:
  6.5 0.0 all-gather.3.cloned.1.call-start
  6.5 1.4 stack.2
  7.9 77.9 %all_to_all.24 = bf16[8,48,4096]{2,1,0:T(8,128)(2,1)} all-to-all(bf16[8,48,4096]{2,1,0:T(8,128)(2,1)S(1)} %stack.2), channel_id=1, replica_groups=mesh['rep'=2,'gx'=8,'gy'=2] {'gx'}, dimensions={0} | all-to-all | bytes 6291456 | tf_op jit(solution)/shard_map/all_to_all | solution.py:20
  85.8 0.0 all-gather.3.cloned.1.call-update
  85.8 0.0 all-gather.5.cloned.1.call-start
  85.9 15.9 %all-gather.3.cloned.1.call-done = bf16[384,8192]{1,0:T(8,128)(2,1)} async-done(((bf16[384,4096]{1,0:T(8,128)(2,1)}), bf16[384,8192]{1,0:T(8,128)(2,1)}) %all-gather.3.cloned.1.call-update) | async-done | bytes 6291472 | tf_op jit(solution)/shard_map/all_gather | solution.py:24
  101.8 0.0 copy-start
  101.8 17.7 %fusion.4 = f32[384,1664]{1,0:T(8,128)S(1)} fusion(bf16[384,8192]{1,0:T(8,128)(2,1)} %all-gather.3.cloned.1.call-done, bf16[8192,1,1664]{2,0,1:T(8,128)(2,1)} %param.7), kind=kOutput, calls=%fused_computation.5 | convolution fusion | flops 10468982784 | bytes 36110336 | tf_op jit(solution)/shard_map/dot_general | solution.py:29
  119.4 0.0 copy-done
  119.5 0.0 copy-start.2
  119.5 0.0 copy-start.1
  119.5 16.7 %fusion.9 = bf16[384,1664]{1,0:T(8,128)(2,1)} fusion(bf16[384,8192]{1,0:T(8,128)(2,1)S(1)} %copy-done, bf16[8192,1,1664]{2,0,1:T(8,128)(2,1)} %param.8, f32[384,1664]{1,0:T(8,128)S(1)} %fusion.4), kind=kOutput, calls=%fused_computation.8 | convolution fusion | flops 10472816640 | bytes 37388288 | tf_op jit(solution)/shard_map/dot_general | solution.py:30
  136.2 0.0 all-gather.5.cloned.1.call-update
  136.2 0.0 reduce-scatter.2.cloned.1.call-start
  136.2 0.0 copy-done.2
  136.3 0.6 dynamic-slice
  137.5 0.0 copy-done.1
  137.5 0.2 dynamic-update-slice
  137.8 11.6 %all-reduce = s32[384]{0:T(512)S(1)} all-reduce(s32[384]{0:T(512)S(1)} %dynamic-update-slice), channel_id=1, replica_groups=mesh['rep'=2,'gx'=8,'gy'=2] {'gx'}, use_global_device_ids=true, to_apply=%add | all-reduce | flops 384 | bytes 3072
  149.4 0.3 reduce-window.24
  149.7 0.1 slice.16
  149.8 0.3 reduce-window.16
  150.1 0.1 slice.14
  150.2 0.1 slice_reduce_fusion
  150.4 0.1 compare_select_fusion
  150.5 134.0 %all-gather.5.cloned.1.call-done = bf16[384,13312]{1,0:T(8,128)(2,1)} async-done(((bf16[384,1664]{1,0:T(8,128)(2,1)}), bf16[384,13312]{1,0:T(8,128)(2,1)}) %all-gather.5.cloned.1.call-update) | async-done | bytes 10223632 | tf_op jit(solution)/shard_map/all_gather | solution.py:33
  284.5 17.4 %fusion = f32[384,1024]{1,0:T(8,128)S(1)} fusion(bf16[384,13312]{1,0:T(8,128)(2,1)} %all-gather.5.cloned.1.call-done, bf16[1,13312,1024]{2,1,0:T(8,128)(2,1)} %param.9), kind=kOutput, calls=%fused_computation.1 | convolution fusion | flops 10468982784 | bytes 39059456 | tf_op jit(solution)/shard_map/dot_general | solution.py:32
  301.8 2.2 scatter_custom_fusion
  304.1 39.6 %all_to_all.25 = f32[8,48,1024]{2,1,0:T(8,128)S(1)} all-to-all(f32[8,48,1024]{2,1,0:T(8,128)S(1)} %bitcast.34), channel_id=1, replica_groups=mesh['rep'=2,'gx'=8,'gy'=2] {'gx'}, dimensions={0} | all-to-all | bytes 3145728 | tf_op jit(solution)/shard_map/all_to_all | solution.py:38
  343.6 1.3 copy.7
  344.9 0.0 reduce-scatter.2.cloned.1.call-update
  344.9 8.1 %reduce-scatter.2.cloned.1.call-done = f32[48,4096]{1,0:T(8,128)} async-done(((f32[48,8192]{1,0:T(8,128)}), f32[48,4096]{1,0:T(8,128)}) %reduce-scatter.2.cloned.1.call-update) | async-done | bytes 786448 | tf_op jit(solution)/shard_map/reduce_scatter | solution.py:39
  353.0 1.9 convert_element_type.7
  (4 shorter events, 0.1 us)
Async XLA Ops:
  6.5 95.2 %all-gather.3.cloned.1.call-start = ((), (), s32[]{:S(2)}) async-start(), calls=%async_computation.3 | async-start | bytes 9437184 | tf_op jit(solution)/shard_map/all_gather | solution.py:24
  85.8 198.6 %all-gather.5.cloned.1.call-start = ((), (), s32[]{:S(2)}) async-start(), calls=%async_computation.4 | async-start | bytes 11501568 | tf_op jit(solution)/shard_map/all_gather | solution.py:33
  101.8 17.7 %copy-start = (bf16[384,8192]{1,0:T(8,128)(2,1)S(1)}, bf16[384,8192]{1,0:T(8,128)(2,1)}, u32[]{:S(2)}) copy-start(bf16[384,8192]{1,0:T(8,128)(2,1)} %all-gather.3.cloned.1.call-done) | copy-start | bytes 18874372
  119.5 16.8 %copy-start.2 = (u32[32]{0:T(128)S(1)}, u32[32]{0:T(128)}, u32[]{:S(2)}) copy-start(u32[32]{0:T(128)} %constant.26) | copy-start | bytes 388
  119.5 18.0 %copy-start.1 = (s32[48]{0:T(128)S(1)}, s32[48]{0:T(128)}, u32[]{:S(2)}) copy-start(s32[48]{0:T(128)} %param.6) | copy-start | bytes 580
  136.2 216.8 %reduce-scatter.2.cloned.1.call-start = ((), (), s32[]{:S(2)}) async-start(), calls=%async_computation.5 | async-start | bytes 2359296 | tf_op jit(solution)/shard_map/reduce_scatter | solution.py:39
Sparse Core Ops, SparseCore 0:
  85.9 15.7 all-gather.2
  136.3 148.1 all-gather.4
  345.0 7.9 reduce-scatter.1

commit v2 on v0

--- a/solution.py
+++ b/solution.py
@@ -33,7 +33,10 @@
         preferred_element_type=jnp.float32,
     )
     placed = jnp.zeros_like(partial_value).at[target].set(partial_value)
-    switched = lax.all_to_all(placed, "gx", split_axis=0, concat_axis=1, tiled=True)
+    switched = jnp.concatenate(
+        lax.all_to_all(jnp.stack(jnp.split(placed, lax.axis_size("gx"), axis=0)), "gx", 0, 0),
+        axis=1,
+    )
     return lax.psum_scatter(switched, "gy", scatter_dimension=1, tiled=True).astype(jnp.bfloat16)
 
 

time: 349 us -> 349 us (level)
  no operation moved by 1% of the time
where the time goes in v2:
time: 349 us
  waiting for transfers between devices  225 us (64%)
  matrix products  51.7 us (15%)
  blocking collectives  51.2 us (15%)
  between operations  13.9 us (4%)
  local copies, waits for them, and re-layouts  4.74 us (1%)
    all_gather x1, waiting for transfers between devices, local(): lax.all_gather(hidden, 'gx', axis=1, tiled=True)  134 us
    all_gather x1, waiting for transfers between devices, local(): lax.all_gather(tokens, 'gx', axis=0, tiled=True)  65 us
    all_to_all x1, blocking collectives, local(): lax.all_to_all(jnp.stack(jnp.split(placed, lax.axis_size('gx'), axis=0)),...  39.6 us
    dot_general x1, matrix products, local(): jnp.dot(gathered, gate_local, preferred_element_type=jnp.float32)  17.7 us
    dot_general x1, matrix products, local(): jnp.dot(lax.all_gather(hidden, 'gx', axis=1, tiled=True), down_local, pre...  17.4 us
    all_gather x1, waiting for transfers between devices, local(): gathered = lax.all_gather(half_rows, 'gy', axis=1, tiled=True)  16.9 us
    dot_general x1, matrix products, local(): up_value = jnp.dot(gathered, up_local, preferred_element_type=jnp.float32)  16.7 us
    unnamed x1, blocking collectives  11.6 us
  transfers between devices with their start and end apart: 4, of which 4 were waited for; matrix products, arithmetic and copies ran while one was open for 1% of the time, Pallas kernels for 0%

profile of v2, /device:TPU:0, one launch (start us, length us, event | category | flops | bytes accessed | tf_op | source)
XLA Modules:
  0.0 349.2 jit_solution(16798101019915804254)
XLA Ops:
  6.5 0.0 all-gather.4.cloned.1.call-start
  6.5 0.7 all-gather.4.cloned.1.call-update
  7.3 0.0 all-gather.6.cloned.1.call-start
  7.3 65.0 %all-gather.4.cloned.1.call-done = bf16[384,4096]{1,0:T(8,128)(2,1)} async-done(((bf16[48,4096]{1,0:T(8,128)(2,1)}), bf16[384,4096]{1,0:T(8,128)(2,1)}) %all-gather.4.cloned.1.call-update) | async-done | bytes 3145744 | tf_op jit(solution)/shard_map/all_gather | solution.py:19
  72.3 0.0 all-gather.6.cloned.1.call-update
  72.3 0.0 all-gather.8.cloned.1.call-start
  72.4 16.9 %all-gather.6.cloned.1.call-done = bf16[384,8192]{1,0:T(8,128)(2,1)} async-done(((bf16[384,4096]{1,0:T(8,128)(2,1)}), bf16[384,8192]{1,0:T(8,128)(2,1)}) %all-gather.6.cloned.1.call-update) | async-done | bytes 6291472 | tf_op jit(solution)/shard_map/all_gather | solution.py:22
  89.3 0.0 copy-start
  89.3 17.7 %fusion.4 = f32[384,1664]{1,0:T(8,128)S(1)} fusion(bf16[384,8192]{1,0:T(8,128)(2,1)} %all-gather.6.cloned.1.call-done, bf16[8192,1,1664]{2,0,1:T(8,128)(2,1)} %param.7), kind=kOutput, calls=%fused_computation.5 | convolution fusion | flops 10468982784 | bytes 36110336 | tf_op jit(solution)/shard_map/dot_general | solution.py:27
  107.0 0.0 copy-done
  107.0 0.0 copy-start.2
  107.0 0.0 copy-start.1
  107.0 16.7 %fusion.9 = bf16[384,1664]{1,0:T(8,128)(2,1)} fusion(bf16[384,8192]{1,0:T(8,128)(2,1)S(1)} %copy-done, bf16[8192,1,1664]{2,0,1:T(8,128)(2,1)} %param.8, f32[384,1664]{1,0:T(8,128)S(1)} %fusion.4), kind=kOutput, calls=%fused_computation.8 | convolution fusion | flops 10472816640 | bytes 37388288 | tf_op jit(solution)/shard_map/dot_general | solution.py:28
  123.7 0.0 all-gather.8.cloned.1.call-update
  123.7 0.0 reduce-scatter.2.cloned.1.call-start
  123.8 0.0 copy-done.2
  123.8 0.6 dynamic-slice
  125.0 0.0 copy-done.1
  125.0 0.2 dynamic-update-slice
  125.3 11.6 %all-reduce = s32[384]{0:T(512)S(1)} all-reduce(s32[384]{0:T(512)S(1)} %dynamic-update-slice), channel_id=1, replica_groups=mesh['rep'=2,'gx'=8,'gy'=2] {'gx'}, use_global_device_ids=true, to_apply=%add | all-reduce | flops 384 | bytes 3072
  136.9 0.3 reduce-window.24
  137.2 0.1 slice.16
  137.3 0.3 reduce-window.16
  137.6 0.1 slice.14
  137.8 0.1 slice_reduce_fusion
  137.9 0.1 compare_select_fusion
  138.0 134.0 %all-gather.8.cloned.1.call-done = bf16[384,13312]{1,0:T(8,128)(2,1)} async-done(((bf16[384,1664]{1,0:T(8,128)(2,1)}), bf16[384,13312]{1,0:T(8,128)(2,1)}) %all-gather.8.cloned.1.call-update) | async-done | bytes 10223632 | tf_op jit(solution)/shard_map/all_gather | solution.py:31
  272.0 17.4 %fusion = f32[384,1024]{1,0:T(8,128)S(1)} fusion(bf16[384,13312]{1,0:T(8,128)(2,1)} %all-gather.8.cloned.1.call-done, bf16[1,13312,1024]{2,1,0:T(8,128)(2,1)} %param.9), kind=kOutput, calls=%fused_computation.1 | convolution fusion | flops 10468982784 | bytes 39059456 | tf_op jit(solution)/shard_map/dot_general | solution.py:30
  289.4 2.2 scatter_custom_fusion
  291.8 39.6 %all_to_all.5 = f32[8,48,1024]{2,1,0:T(8,128)S(1)} all-to-all(f32[8,48,1024]{2,1,0:T(8,128)S(1)} %fusion.14), channel_id=1, replica_groups=mesh['rep'=2,'gx'=8,'gy'=2] {'gx'}, dimensions={0} | all-to-all | bytes 3145728 | tf_op jit(solution)/shard_map/all_to_all | solution.py:37
  331.3 1.3 copy.21
  332.6 0.0 reduce-scatter.2.cloned.1.call-update
  332.6 8.1 %reduce-scatter.2.cloned.1.call-done = f32[48,4096]{1,0:T(8,128)} async-done(((f32[48,8192]{1,0:T(8,128)}), f32[48,4096]{1,0:T(8,128)}) %reduce-scatter.2.cloned.1.call-update) | async-done | bytes 786448 | tf_op jit(solution)/shard_map/reduce_scatter | solution.py:40
  340.7 1.9 convert_element_type.7
  (12 shorter events, 0.2 us)
Async XLA Ops:
  6.5 65.7 %all-gather.4.cloned.1.call-start = ((), (), s32[]{:S(2)}) async-start(), calls=%async_computation.2 | async-start | bytes 3538944 | tf_op jit(solution)/shard_map/all_gather | solution.py:19
  7.3 82.0 %all-gather.6.cloned.1.call-start = ((), (), s32[]{:S(2)}) async-start(), calls=%async_computation.3 | async-start | bytes 9437184 | tf_op jit(solution)/shard_map/all_gather | solution.py:22
  72.3 199.7 %all-gather.8.cloned.1.call-start = ((), (), s32[]{:S(2)}) async-start(), calls=%async_computation.4 | async-start | bytes 11501568 | tf_op jit(solution)/shard_map/all_gather | solution.py:31
  89.3 17.7 %copy-start = (bf16[384,8192]{1,0:T(8,128)(2,1)S(1)}, bf16[384,8192]{1,0:T(8,128)(2,1)}, u32[]{:S(2)}) copy-start(bf16[384,8192]{1,0:T(8,128)(2,1)} %all-gather.6.cloned.1.call-done) | copy-start | bytes 18874372
  107.0 16.8 %copy-start.2 = (u32[32]{0:T(128)S(1)}, u32[32]{0:T(128)}, u32[]{:S(2)}) copy-start(u32[32]{0:T(128)} %constant.26) | copy-start | bytes 388
  107.0 18.0 %copy-start.1 = (s32[48]{0:T(128)S(1)}, s32[48]{0:T(128)}, u32[]{:S(2)}) copy-start(s32[48]{0:T(128)} %param.6) | copy-start | bytes 580
  123.7 217.0 %reduce-scatter.2.cloned.1.call-start = ((), (), s32[]{:S(2)}) async-start(), calls=%async_computation.5 | async-start | bytes 2359296 | tf_op jit(solution)/shard_map/reduce_scatter | solution.py:40
Sparse Core Ops, SparseCore 0:
  9.5 62.7 all-gather.3
  73.8 15.4 all-gather.5
  123.8 148.1 all-gather.7
  332.7 7.9 reduce-scatter.1
